TPU v7x, 32 devices: a whole 2x2x4 slice. The times are simulated.
32 devices in a mesh: gz: 16 (over z, y, x), gy: 2 (over core).
Axes of the slice: x: 2, y: 2, z: 4, core: 2. Of those that a mesh axis runs over, the one named last changes fastest.
Arguments:
- snapshots: float32 [48, 64, 128, 256], P(None, 'gz', 'gy'), may hold values from -6 to 6
- energies: float32 [48], replicated, may hold values from 0.3 to 3
- plane_weight: float32 [64], P('gz'), may hold values from 1 to 10
Outputs:
- modes: float32 [16, 64, 128, 256], P(None, 'gz', 'gy')
- basis: float32 [48, 16], replicated
All inputs are finite; a program needn't handle non-finite values.
Results may differ from a plain program's by a relative error of at most 0.0003.
Values sent between devices are 32-bit elements; how exact they have to be, the bound alone decides.
A program may use at most 128 MiB of HBM per device.

v0:
```python
import jax
import jax.numpy as jnp
from jax import lax
from jax.sharding import PartitionSpec as P

MODES = 16
ITERS = 6


def padded_2(block, sides, width):
    for axis, dim in sides:
        count = lax.axis_size(axis)
        forward = [(i, i + 1) for i in range(count - 1)]
        forward.append((count - 1, 0))
        backward = [(target, source) for source, target in forward]
        low = lax.ppermute(
            lax.slice_in_dim(block, block.shape[dim] - width, None, axis=dim), axis, forward
        )
        high = lax.ppermute(lax.slice_in_dim(block, 0, width, axis=dim), axis, backward)
        block = jnp.concatenate([low, block, high], axis=dim)
    return block


def local(snapshots, energies, plane_weight):
    count, planes, rows, width = snapshots.shape
    total = planes * lax.axis_size("gz") * rows * lax.axis_size("gy") * width
    scaled = snapshots * energies[:, None, None, None]
    padded = padded_2(scaled, (("gz", 1),), 1)
    filtered = 0.25 * padded[:, :-2] + 0.5 * scaled + 0.25 * padded[:, 2:]
    flat = filtered.reshape(count, -1)
    weighted = (filtered * plane_weight[None, :, None, None]).reshape(count, -1)
    partial_value = jnp.dot(weighted, flat.T, precision=lax.Precision.HIGHEST) / total
    gram = lax.psum(partial_value, ("gz", "gy"))
    basis = jnp.eye(count, dtype=jnp.float32)[:, :MODES]
    for step in range(ITERS):
        image = jnp.dot(gram, basis, precision=lax.Precision.HIGHEST)
        factor = jnp.linalg.cholesky(jnp.dot(image.T, image, precision=lax.Precision.HIGHEST))
        basis = jax.scipy.linalg.solve_triangular(factor, image.T, lower=True).T
    raw = jnp.dot(basis.T, flat, precision=lax.Precision.HIGHEST).reshape(
        MODES, planes, rows, width
    )
    projected = jnp.dot(gram, basis, precision=lax.Precision.HIGHEST)
    norms = jnp.sum(basis * projected, axis=0)
    modes = raw / jnp.sqrt(norms)[:, None, None, None]
    return (modes, basis)


def solution(mesh):
    placed = (P(None, "gz", "gy", None), P(), P("gz"))
    return jax.shard_map(
        local,
        mesh=mesh,
        in_specs=placed,
        out_specs=(P(None, "gz", "gy", None), P()),
        check_vma=False,
    )
```

profile of v0, /device:TPU:0, one launch (start us, length us, event | category | flops | bytes accessed | tf_op | source)
XLA Modules:
  0.0 292.3 jit_solution(18266743144551200550)
XLA Ops:
  0.6 12.0 %broadcast_multiply_fusion.1 = f32[48,4,64,256]{3,2,1,0:T(8,128)} fusion(f32[48,4,64,256]{3,2,1,0:T(8,128)} %param.6, f32[48]{0:T(128)} %param.7), kind=kLoop, calls=%fused_computation.12 | loop fusion | flops 3145728 | bytes 25166016 | tf_op jit(solution)/shard_map/mul | solution.py:27
  12.7 0.0 copy-start
  12.7 3.7 %fusion.67 = (f32[48,1,64,256]{3,2,1,0:T(8,128)S(1)}, f32[48,1,64,256]{3,2,1,0:T(8,128)S(1)}) fusion(f32[48,4,64,256]{3,2,1,0:T(8,128)} %broadcast_multiply_fusion.1), kind=kLoop, calls=%fused_computation.84 | loop fusion | bytes 12582912 | tf_op jit(solution)/shard_map/slice | solution.py:17
  16.4 3.0 %collective-permute-start = (f32[48,1,64,256]{3,2,1,0:T(8,128)S(1)}, f32[48,1,64,256]{3,2,1,0:T(8,128)}, u32[]{:S(2)}, u32[]{:S(2)}) collective-permute-start(f32[48,1,64,256]{3,2,1,0:T(8,128)S(1)} %get-tuple-element.10), channel_id=1, source_target_pairs={{0,2},{2,4},{4,6},{6,8},{8,10},{10,12},{12,14},{14,16},{16,18},{18... | collective-permute-start | bytes 9437192 | tf_op jit(solution)/shard_map/ppermute | solution.py:16
  19.4 4.1 %collective-permute-start.1 = (f32[48,1,64,256]{3,2,1,0:T(8,128)S(1)}, f32[48,1,64,256]{3,2,1,0:T(8,128)}, u32[]{:S(2)}, u32[]{:S(2)}) collective-permute-start(f32[48,1,64,256]{3,2,1,0:T(8,128)S(1)} %get-tuple-element.11), channel_id=1, source_target_pairs={{2,0},{4,2},{6,4},{8,6},{10,8},{12,10},{14,12},{16,14},{18,16},{20... | collective-permute-start | bytes 9437192 | tf_op jit(solution)/shard_map/ppermute | solution.py:19
  23.5 130.7 %collective-permute-done = f32[48,1,64,256]{3,2,1,0:T(8,128)} collective-permute-done((f32[48,1,64,256]{3,2,1,0:T(8,128)S(1)}, f32[48,1,64,256]{3,2,1,0:T(8,128)}, u32[]{:S(2)}, u32[]{:S(2)}) %collective-permute-start) | collective-permute-done | bytes 3145760 | tf_op jit(solution)/shard_map/ppermute | solution.py:16
  154.2 2.1 collective-permute-done.1
  156.2 0.0 copy-done
  156.2 0.0 copy-done.2
  156.3 13.5 %broadcast_multiply_fusion = (f32[48,4,64,256]{3,2,1,0:T(8,128)}, f32[48,4,64,256]{3,2,1,0:T(8,128)}) fusion(f32[4]{0:T(128)S(1)} %copy-done.2, f32[48,1,64,256]{3,2,1,0:T(8,128)} %collective-permute-done.1, f32[48,4,64,256]{3,2,1,0:T(8,128)S(1)} %copy-done, f32[48,1,64,256]{3,2,1,0:T(8,128)} %collective-permute-done), kind=kLoop, calls=%fused_computation.11 | loop fusion | flops 25165824 | bytes 44040208 | tf_op jit(solution)/shard_map/mul | solution.py:31
  169.7 32.1 %fusion.16 = f32[48,48]{1,0:T(8,128)S(1)} fusion(f32[48,4,64,256]{3,2,1,0:T(8,128)} %get-tuple-element.9, f32[48,4,64,256]{3,2,1,0:T(8,128)} %get-tuple-element.8), kind=kOutput, calls=%fused_computation.15 | convolution fusion | flops 1811941632 | bytes 25175040 | tf_op jit(solution)/shard_map/dot_general | solution.py:32
  201.8 39.7 %psum.7 = f32[48,48]{1,0:T(8,128)S(1)} all-reduce(f32[48,48]{1,0:T(8,128)S(1)} %fusion.16), channel_id=1, replica_groups=mesh['gz'=16,'gy'=2] {'gz','gy'}, use_global_device_ids=true, to_apply=%region_0.0 | all-reduce | flops 2304 | bytes 18432 | tf_op jit(solution)/shard_map/psum | solution.py:33
  241.6 0.2 fusion.22
  241.8 0.1 fusion.68
  241.9 0.1 copy.16
  242.0 1.5 cholesky.104
  243.5 0.6 compare_reduce_fusion.5
  244.1 0.6 fusion.24
  244.8 1.2 custom-call.10
  246.0 0.2 fusion.51
  246.2 0.2 fusion.69
  246.4 0.1 fusion.70
  246.5 0.1 copy.17
  246.6 1.5 cholesky.115
  248.1 0.6 compare_reduce_fusion.4
  248.8 0.6 fusion.25
  249.4 1.2 custom-call.11
  250.6 0.2 fusion.47
  250.8 0.2 fusion.71
  251.0 0.1 fusion.72
  251.1 0.1 copy.18
  251.2 1.5 cholesky.126
  252.7 0.6 compare_reduce_fusion.3
  253.4 0.6 fusion.26
  254.0 1.2 custom-call.12
  255.3 0.2 fusion.43
  255.5 0.2 fusion.73
  255.6 0.1 fusion.74
  255.8 0.1 copy.19
  255.8 1.5 cholesky.137
  257.4 0.6 compare_reduce_fusion.2
  258.0 0.6 fusion.27
  258.7 1.2 custom-call.13
  259.9 0.2 fusion.39
  260.1 0.2 fusion.75
  260.2 0.1 fusion.76
  260.4 0.1 copy.20
  260.5 1.5 cholesky.148
  262.0 0.6 compare_reduce_fusion.1
  262.6 0.6 fusion.28
  263.3 1.2 custom-call.14
  264.5 0.2 fusion.35
  264.7 0.2 fusion.77
  264.9 0.1 fusion.78
  265.0 0.1 copy.21
  265.1 1.5 cholesky.159
  266.6 0.6 compare_reduce_fusion
  267.2 0.6 fusion.29
  267.9 1.2 custom-call.15
  269.1 0.2 fusion.31
  269.3 0.3 fusion.21
  269.6 18.2 %broadcast_divide_fusion = f32[16,4,64,256]{3,0,2,1:T(8,128)S(1)} fusion(f32[16]{0:T(128)S(1)} %sqrt.7, f32[4,64,256,48]{2,1,0,3:T(8,128)} %bitcast.120, f32[16,48]{1,0:T(8,128)S(1)} %fusion.31), kind=kOutput, calls=%fused_computation.13 | convolution fusion | flops 605028352 | bytes 16780352 | tf_op jit(solution)/shard_map/dot_general | solution.py:39
  287.8 4.4 %copy.23 = f32[16,4,64,256]{3,2,1,0:T(8,128)} copy(f32[16,4,64,256]{3,0,2,1:T(8,128)S(1)} %broadcast_divide_fusion) | data formatting | bytes 8388608
  292.3 0.0 copy-done.1
  (15 shorter events, 0.2 us)
Async XLA Ops:
  12.7 143.6 %copy-start = (f32[48,4,64,256]{3,2,1,0:T(8,128)S(1)}, f32[48,4,64,256]{3,2,1,0:T(8,128)}, u32[]{:S(2)}) copy-start(f32[48,4,64,256]{3,2,1,0:T(8,128)} %broadcast_multiply_fusion.1) | copy-start | bytes 37748740
  12.7 143.6 %copy-start.2 = (f32[4]{0:T(128)S(1)}, f32[4]{0:T(128)}, u32[]{:S(2)}) copy-start(f32[4]{0:T(128)} %param.8) | copy-start | bytes 52
  16.4 137.8 %collective-permute-start = (f32[48,1,64,256]{3,2,1,0:T(8,128)S(1)}, f32[48,1,64,256]{3,2,1,0:T(8,128)}, u32[]{:S(2)}, u32[]{:S(2)}) collective-permute-start(f32[48,1,64,256]{3,2,1,0:T(8,128)S(1)} %get-tuple-element.10), channel_id=1, source_target_pairs={{0,2},{2,4},{4,6},{6,8},{8,10},{10,12},{12,14},{14,16},{16,18},{18... | collective-permute-start | bytes 9437192 | tf_op jit(solution)/shard_map/ppermute | solution.py:16
  19.4 136.8 %collective-permute-start.1 = (f32[48,1,64,256]{3,2,1,0:T(8,128)S(1)}, f32[48,1,64,256]{3,2,1,0:T(8,128)}, u32[]{:S(2)}, u32[]{:S(2)}) collective-permute-start(f32[48,1,64,256]{3,2,1,0:T(8,128)S(1)} %get-tuple-element.11), channel_id=1, source_target_pairs={{2,0},{4,2},{6,4},{8,6},{10,8},{12,10},{14,12},{16,14},{18,16},{20... | collective-permute-start | bytes 9437192 | tf_op jit(solution)/shard_map/ppermute | solution.py:19
  269.3 22.9 %copy-start.1 = (f32[16,48]{1,0:T(8,128)}, f32[16,48]{1,0:T(8,128)S(1)}, u32[]{:S(2)}) copy-start(f32[16,48]{1,0:T(8,128)S(1)} %fusion.31) | copy-start | bytes 9220
where the time goes:
time: 293 us; the launch traced here: 292 us
  waiting for transfers between devices  133 us (45%)
  matrix products  53.6 us (18%)
  other arithmetic  49.7 us (17%)
  blocking collectives  39.7 us (14%)
  local copies, waits for them, and re-layouts  8.63 us (3%)
  starting transfers between devices  7.08 us (2%)
    ppermute x1, waiting for transfers between devices, padded_2(): lax.ppermute(lax.slice_in_dim(block, block.shape[dim] - width, None, axis...  131 us
    psum x1, blocking collectives, local(): gram = lax.psum(partial_value, ('gz', 'gy'))  39.7 us
    dot_general x1, matrix products, local(): jnp.dot(weighted, flat.T, precision=lax.Precision.HIGHEST) / total  32.1 us
    dot_general x1, matrix products, local(): jnp.dot(basis.T, flat, precision=lax.Precision.HIGHEST)  18.2 us
    mul x1, other arithmetic, local(): weighted = (filtered * plane_weight[None, :, None, None]).reshape(count, -1)  13.5 us
    another operation x18, other arithmetic, local(): jnp.linalg.cholesky(jnp.dot(image.T, image, precision=lax.Precision.HIGHE...  12.9 us
    mul x1, other arithmetic, local(): scaled = snapshots * energies[:, None, None, None]  12 us
    another operation x12, other arithmetic, local(): basis = jax.scipy.linalg.solve_triangular(factor, image.T, lower=True).T  11.3 us
  transfers between devices with their start and end apart: 2, of which 2 were waited for; matrix products, arithmetic and copies ran while one was open for 0% of the time, Pallas kernels for 0%

commit v1 on v0

--- a/solution.py
+++ b/solution.py
@@ -30,7 +30,7 @@
     flat = filtered.reshape(count, -1)
     weighted = (filtered * plane_weight[None, :, None, None]).reshape(count, -1)
     partial_value = jnp.dot(weighted, flat.T, precision=lax.Precision.HIGHEST) / total
-    gram = lax.psum(partial_value, ("gz", "gy"))
+    gram = lax.psum(lax.psum(partial_value, "gy"), "gz")
     basis = jnp.eye(count, dtype=jnp.float32)[:, :MODES]
     for step in range(ITERS):
         image = jnp.dot(gram, basis, precision=lax.Precision.HIGHEST)

time: 293 us -> 331 us (1.13)
  blocking collectives: 39.7 us -> 78.3 us
    psum x1 -> x2, blocking collectives: 39.7 us -> 78.3 us  [local(): gram = lax.psum(lax.psum(partial_value, 'gy'), 'gz')]
where the time goes in v1:
time: 331 us
  waiting for transfers between devices  133 us (40%)
  blocking collectives  78.3 us (24%)
  matrix products  53.6 us (16%)
  other arithmetic  49.7 us (15%)
  local copies, waits for them, and re-layouts  8.63 us (3%)
  starting transfers between devices  7.08 us (2%)
    ppermute x1, waiting for transfers between devices, padded_2(): lax.ppermute(lax.slice_in_dim(block, block.shape[dim] - width, None, axis...  131 us
    psum x2, blocking collectives, local(): gram = lax.psum(lax.psum(partial_value, 'gy'), 'gz')  78.3 us
    dot_general x1, matrix products, local(): jnp.dot(weighted, flat.T, precision=lax.Precision.HIGHEST) / total  32.1 us
    dot_general x1, matrix products, local(): jnp.dot(basis.T, flat, precision=lax.Precision.HIGHEST)  18.2 us
    mul x1, other arithmetic, local(): weighted = (filtered * plane_weight[None, :, None, None]).reshape(count, -1)  13.5 us
    another operation x18, other arithmetic, local(): jnp.linalg.cholesky(jnp.dot(image.T, image, precision=lax.Precision.HIGHE...  12.9 us
    mul x1, other arithmetic, local(): scaled = snapshots * energies[:, None, None, None]  12 us
    another operation x12, other arithmetic, local(): basis = jax.scipy.linalg.solve_triangular(factor, image.T, lower=True).T  11.3 us
  transfers between devices with their start and end apart: 2, of which 2 were waited for; matrix products, arithmetic and copies ran while one was open for 0% of the time, Pallas kernels for 0%

profile of v1, /device:TPU:0, one launch (start us, length us, event | category | flops | bytes accessed | tf_op | source)
XLA Modules:
  0.0 330.9 jit_solution(10026306394363154525)
XLA Ops:
  0.6 12.0 %broadcast_multiply_fusion.1 = f32[48,4,64,256]{3,2,1,0:T(8,128)} fusion(f32[48,4,64,256]{3,2,1,0:T(8,128)} %param.6, f32[48]{0:T(128)} %param.7), kind=kLoop, calls=%fused_computation.12 | loop fusion | flops 3145728 | bytes 25166016 | tf_op jit(solution)/shard_map/mul | solution.py:27
  12.7 3.7 %fusion.67 = (f32[48,1,64,256]{3,2,1,0:T(8,128)S(1)}, f32[48,1,64,256]{3,2,1,0:T(8,128)S(1)}) fusion(f32[48,4,64,256]{3,2,1,0:T(8,128)} %broadcast_multiply_fusion.1), kind=kLoop, calls=%fused_computation.84 | loop fusion | bytes 12582912 | tf_op jit(solution)/shard_map/slice | solution.py:17
  16.4 3.0 collective-permute-start
  19.4 4.1 %collective-permute-start.1 = (f32[48,1,64,256]{3,2,1,0:T(8,128)S(1)}, f32[48,1,64,256]{3,2,1,0:T(8,128)}, u32[]{:S(2)}, u32[]{:S(2)}) collective-permute-start(f32[48,1,64,256]{3,2,1,0:T(8,128)S(1)} %get-tuple-element.11), channel_id=1, source_target_pairs={{2,0},{4,2},{6,4},{8,6},{10,8},{12,10},{14,12},{16,14},{18,16},{20... | collective-permute-start | bytes 9437192 | tf_op jit(solution)/shard_map/ppermute | solution.py:19
  23.5 130.7 %collective-permute-done = f32[48,1,64,256]{3,2,1,0:T(8,128)} collective-permute-done((f32[48,1,64,256]{3,2,1,0:T(8,128)S(1)}, f32[48,1,64,256]{3,2,1,0:T(8,128)}, u32[]{:S(2)}, u32[]{:S(2)}) %collective-permute-start) | collective-permute-done | bytes 3145760 | tf_op jit(solution)/shard_map/ppermute | solution.py:16
  154.2 2.1 collective-permute-done.1
  156.2 0.0 copy-done
  156.2 0.0 copy-done.2
  156.3 13.5 %broadcast_multiply_fusion = (f32[48,4,64,256]{3,2,1,0:T(8,128)}, f32[48,4,64,256]{3,2,1,0:T(8,128)}) fusion(f32[4]{0:T(128)S(1)} %copy-done.2, f32[48,1,64,256]{3,2,1,0:T(8,128)} %collective-permute-done.1, f32[48,4,64,256]{3,2,1,0:T(8,128)S(1)} %copy-done, f32[48,1,64,256]{3,2,1,0:T(8,128)} %collective-permute-done), kind=kLoop, calls=%fused_computation.11 | loop fusion | flops 25165824 | bytes 44040208 | tf_op jit(solution)/shard_map/mul | solution.py:31
  169.7 32.1 %fusion.16 = f32[48,48]{1,0:T(8,128)S(1)} fusion(f32[48,4,64,256]{3,2,1,0:T(8,128)} %get-tuple-element.9, f32[48,4,64,256]{3,2,1,0:T(8,128)} %get-tuple-element.8), kind=kOutput, calls=%fused_computation.15 | convolution fusion | flops 1811941632 | bytes 25175040 | tf_op jit(solution)/shard_map/dot_general | solution.py:32
  201.8 3.4 %psum.14 = f32[48,48]{1,0:T(8,128)S(1)} all-reduce(f32[48,48]{1,0:T(8,128)S(1)} %fusion.16), channel_id=1, replica_groups=mesh['gz'=16,'gy'=2] {'gy'}, use_global_device_ids=true, to_apply=%region_0.0 | all-reduce | flops 2304 | bytes 18432 | tf_op jit(solution)/shard_map/psum | solution.py:33
  205.3 74.9 %psum.15 = f32[48,48]{1,0:T(8,128)S(1)} all-reduce(f32[48,48]{1,0:T(8,128)S(1)} %psum.14), channel_id=1, replica_groups=mesh['gz'=16,'gy'=2] {'gz'}, use_global_device_ids=true, to_apply=%region_1.0 | all-reduce | flops 2304 | bytes 18432 | tf_op jit(solution)/shard_map/psum | solution.py:33
  280.2 0.2 fusion.22
  280.4 0.1 fusion.68
  280.5 0.1 copy.16
  280.6 1.5 cholesky.104
  282.1 0.6 compare_reduce_fusion.5
  282.7 0.6 fusion.24
  283.4 1.2 custom-call.10
  284.6 0.2 fusion.51
  284.8 0.2 fusion.69
  285.0 0.1 fusion.70
  285.1 0.1 copy.17
  285.2 1.5 cholesky.115
  286.7 0.6 compare_reduce_fusion.4
  287.4 0.6 fusion.25
  288.0 1.2 custom-call.11
  289.2 0.2 fusion.47
  289.4 0.2 fusion.71
  289.6 0.1 fusion.72
  289.8 0.1 copy.18
  289.8 1.5 cholesky.126
  291.3 0.6 compare_reduce_fusion.3
  292.0 0.6 fusion.26
  292.6 1.2 custom-call.12
  293.9 0.2 fusion.43
  294.1 0.2 fusion.73
  294.2 0.1 fusion.74
  294.4 0.1 copy.19
  294.5 1.5 cholesky.137
  296.0 0.6 compare_reduce_fusion.2
  296.6 0.6 fusion.27
  297.3 1.2 custom-call.13
  298.5 0.2 fusion.39
  298.7 0.2 fusion.75
  298.8 0.1 fusion.76
  299.0 0.1 copy.20
  299.1 1.5 cholesky.148
  300.6 0.6 compare_reduce_fusion.1
  301.2 0.6 fusion.28
  301.9 1.2 custom-call.14
  303.1 0.2 fusion.35
  303.3 0.2 fusion.77
  303.5 0.1 fusion.78
  303.6 0.1 copy.21
  303.7 1.5 cholesky.159
  305.2 0.6 compare_reduce_fusion
  305.9 0.6 fusion.29
  306.5 1.2 custom-call.15
  307.7 0.2 fusion.31
  307.9 0.3 fusion.21
  308.2 18.2 %broadcast_divide_fusion = f32[16,4,64,256]{3,0,2,1:T(8,128)S(1)} fusion(f32[16]{0:T(128)S(1)} %sqrt.7, f32[4,64,256,48]{2,1,0,3:T(8,128)} %bitcast.120, f32[16,48]{1,0:T(8,128)S(1)} %fusion.31), kind=kOutput, calls=%fused_computation.13 | convolution fusion | flops 605028352 | bytes 16780352 | tf_op jit(solution)/shard_map/dot_general | solution.py:39
  326.4 4.4 %copy.23 = f32[16,4,64,256]{3,2,1,0:T(8,128)} copy(f32[16,4,64,256]{3,0,2,1:T(8,128)S(1)} %broadcast_divide_fusion) | data formatting | bytes 8388608
  330.9 0.0 copy-done.1
  (16 shorter events, 0.2 us)
Async XLA Ops:
  12.7 143.6 %copy-start = (f32[48,4,64,256]{3,2,1,0:T(8,128)S(1)}, f32[48,4,64,256]{3,2,1,0:T(8,128)}, u32[]{:S(2)}) copy-start(f32[48,4,64,256]{3,2,1,0:T(8,128)} %broadcast_multiply_fusion.1) | copy-start | bytes 37748740
  12.7 143.6 %copy-start.2 = (f32[4]{0:T(128)S(1)}, f32[4]{0:T(128)}, u32[]{:S(2)}) copy-start(f32[4]{0:T(128)} %param.8) | copy-start | bytes 52
  16.4 137.8 %collective-permute-start = (f32[48,1,64,256]{3,2,1,0:T(8,128)S(1)}, f32[48,1,64,256]{3,2,1,0:T(8,128)}, u32[]{:S(2)}, u32[]{:S(2)}) collective-permute-start(f32[48,1,64,256]{3,2,1,0:T(8,128)S(1)} %get-tuple-element.10), channel_id=1, source_target_pairs={{0,2},{2,4},{4,6},{6,8},{8,10},{10,12},{12,14},{14,16},{16,18},{18... | collective-permute-start | bytes 9437192 | tf_op jit(solution)/shard_map/ppermute | solution.py:16
  19.4 136.8 %collective-permute-start.1 = (f32[48,1,64,256]{3,2,1,0:T(8,128)S(1)}, f32[48,1,64,256]{3,2,1,0:T(8,128)}, u32[]{:S(2)}, u32[]{:S(2)}) collective-permute-start(f32[48,1,64,256]{3,2,1,0:T(8,128)S(1)} %get-tuple-element.11), channel_id=1, source_target_pairs={{2,0},{4,2},{6,4},{8,6},{10,8},{12,10},{14,12},{16,14},{18,16},{20... | collective-permute-start | bytes 9437192 | tf_op jit(solution)/shard_map/ppermute | solution.py:19
  307.9 22.9 %copy-start.1 = (f32[16,48]{1,0:T(8,128)}, f32[16,48]{1,0:T(8,128)S(1)}, u32[]{:S(2)}) copy-start(f32[16,48]{1,0:T(8,128)S(1)} %fusion.31) | copy-start | bytes 9220
